TPU v7x, 32 devices: a whole 2x2x4 slice. The times are simulated.
32 devices in a mesh: owner: 4 (over z), rows: 8 (over y, x, core).
Axes of the slice: x: 2, y: 2, z: 4, core: 2. Of those that a mesh axis runs over, the one named last changes fastest.
Arguments:
- w_gate: float32 [128, 2048, 768], P('owner', 'rows'), may hold values from -0.1875 to 0.1875
- w_up: float32 [128, 2048, 768], P('owner', 'rows'), may hold values from -0.1875 to 0.1875
- router_weight: float32 [2048, 128], P('rows', 'owner'), may hold values from -0.125 to 0.125
- router_gain: float32 [2048], P('rows'), may hold values from 0.25 to 1.75
Outputs:
- serve_gate: bfloat16 [128, 2048, 768], P('owner', None, 'rows')
- serve_up: bfloat16 [128, 2048, 768], P('owner', None, 'rows')
- scale_gate: float32 [128, 768], P('owner', 'rows')
- scale_up: float32 [128, 768], P('owner', 'rows')
- serve_router: bfloat16 [2048, 128], replicated
All inputs are finite; a program needn't handle non-finite values. Where the computation divides by a largest or mean magnitude, that divisor is 1e-20 or more.
Results may differ from a plain program's by a relative error of at most 0.001.
Values may be sent and summed in bfloat16 or wider, within the bound.
No kernel may reach another device: no remote copies, remote signals or barrier semaphores. Data moves between devices by JAX's collectives and lax.ppermute only.
A program may use at most 192 MiB of HBM per device.

v0:
```python
import jax
import jax.numpy as jnp
from jax import lax
from jax.sharding import PartitionSpec as P

D_MODEL = 2048


def on_device(w_gate, w_up, router_weight, router_gain):
    total_gate, total_up = lax.psum(
        (jnp.sum(jnp.abs(w_gate), axis=1), jnp.sum(jnp.abs(w_up), axis=1)), "rows"
    )
    scale_gate = total_gate / D_MODEL
    scale_up = total_up / D_MODEL
    narrow_gate, narrow_up = (
        (w_gate / jnp.expand_dims(scale_gate, 1)).astype(jnp.bfloat16),
        (w_up / jnp.expand_dims(scale_up, 1)).astype(jnp.bfloat16),
    )
    serve_gate, serve_up = (
        lax.all_to_all(narrow_gate, "rows", split_axis=2, concat_axis=1, tiled=True),
        lax.all_to_all(narrow_up, "rows", split_axis=2, concat_axis=1, tiled=True),
    )
    scale_gate = lax.dynamic_slice_in_dim(
        scale_gate, lax.axis_index("rows") * serve_gate.shape[2], serve_gate.shape[2], axis=1
    )
    scale_up = lax.dynamic_slice_in_dim(
        scale_up, lax.axis_index("rows") * serve_up.shape[2], serve_up.shape[2], axis=1
    )
    part_router = (router_weight * router_gain[:, None]).astype(jnp.bfloat16)
    row_router = lax.all_gather(part_router, "rows", axis=0, tiled=True)
    serve_router = lax.all_gather(row_router, "owner", axis=1, tiled=True)
    return (serve_gate, serve_up, scale_gate, scale_up, serve_router)


def solution(mesh):
    placed = (P("owner", "rows", None), P("owner", "rows", None), P("rows", "owner"), P("rows"))
    return jax.shard_map(
        on_device,
        mesh=mesh,
        in_specs=placed,
        out_specs=(
            P("owner", None, "rows"),
            P("owner", None, "rows"),
            P("owner", "rows"),
            P("owner", "rows"),
            P(),
        ),
        check_vma=False,
    )
```

profile of v0, /device:TPU:0, one launch (start us, length us, event | category | flops | bytes accessed | tf_op | source)
XLA Modules:
  0.0 481.1 jit_solution(11326135817132377053)
XLA Ops:
  7.2 0.0 all-reduce.3.cloned.1.call-start
  7.2 17.4 %abs_reduce_fusion = (f32[32,768]{1,0:T(8,128)}, f32[32,768]{1,0:T(8,128)}) fusion(f32[32,256,768]{2,1,0:T(8,128)} %param.5, f32[32,256,768]{2,1,0:T(8,128)} %param.4), kind=kLoop, calls=%fused_computation.1 | loop fusion | flops 25116672 | bytes 50528256 | tf_op jit(solution)/shard_map/reduce_sum | solution.py:11
  24.6 0.0 all-reduce.3.cloned.1.call-update
  24.7 25.1 %copy.25 = f32[32,256,768]{1,0,2:T(8,128)} copy(f32[32,256,768]{2,1,0:T(8,128)} %param.5) | data formatting | bytes 50331648 | tf_op args[1]
  49.8 31.5 %all-reduce.3.cloned.1.call-done = (f32[32,768]{1,0:T(8,128)}, f32[32,768]{1,0:T(8,128)}) async-done(((f32[32,768]{1,0:T(8,128)}, f32[32,768]{1,0:T(8,128)}), (f32[32,768]{1,0:T(8,128)}, f32[32,768]{1,0:T(8,128)})) %all-reduce.3.cloned.1.call-update) | async-done | bytes 196624 | tf_op jit(solution)/shard_map/psum | solution.py:10
  81.3 0.9 broadcast_multiply_fusion
  82.2 0.2 copy.24
  82.4 14.1 %divide_convert_fusion = bf16[32,256,768]{1,0,2:T(8,128)(2,1)} fusion(f32[32,256,768]{1,0,2:T(8,128)} %copy.25, f32[32,768]{0,1:T(8,128)S(1)} %copy.24), kind=kLoop, calls=%fused_computation | loop fusion | flops 12582912 | bytes 37847040 | tf_op jit(solution)/shard_map/convert_element_type | solution.py:17
  96.5 5.4 %all-to-all-start.1 = ((bf16[32,256,768]{1,0,2:T(8,128)(2,1)}), bf16[32,256,768]{1,0,2:T(8,128)(2,1)}, u32[]{:S(2)}, u32[]{:S(2)}) async-start(bf16[32,256,768]{1,0,2:T(8,128)(2,1)} %divide_convert_fusion), calls=%async_computation.1 | async-start | bytes 25165824 | tf_op jit(solution)/shard_map/all_to_all | solution.py:21
  101.9 25.1 %copy.21 = f32[32,256,768]{1,0,2:T(8,128)} copy(f32[32,256,768]{2,1,0:T(8,128)} %param.4) | data formatting | bytes 50331648 | tf_op args[0]
  127.1 0.2 copy.20
  127.2 0.0 copy-start.1
  127.3 14.1 %divide_convert_fusion.1 = bf16[32,256,768]{1,0,2:T(8,128)(2,1)} fusion(f32[32,256,768]{1,0,2:T(8,128)} %copy.21, f32[32,768]{0,1:T(8,128)S(1)} %copy.20), kind=kLoop, calls=%fused_computation.2 | loop fusion | flops 12582912 | bytes 37847040 | tf_op jit(solution)/shard_map/convert_element_type | solution.py:16
  141.4 99.5 %all-to-all-done.1 = bf16[32,256,768]{1,0,2:T(8,128)(2,1)} async-done(((bf16[32,256,768]{1,0,2:T(8,128)(2,1)}), bf16[32,256,768]{1,0,2:T(8,128)(2,1)}, u32[]{:S(2)}, u32[]{:S(2)}) %all-to-all-start.1) | async-done | bytes 12582944 | tf_op jit(solution)/shard_map/all_to_all | solution.py:21
  240.9 5.4 %all-to-all-start = ((bf16[32,256,768]{1,0,2:T(8,128)(2,1)}), bf16[32,256,768]{1,0,2:T(8,128)(2,1)}, u32[]{:S(2)}, u32[]{:S(2)}) async-start(bf16[32,256,768]{1,0,2:T(8,128)(2,1)} %divide_convert_fusion.1), calls=%async_computation | async-start | bytes 25165824 | tf_op jit(solution)/shard_map/all_to_all | solution.py:20
  246.3 142.4 %all_gather.6 = bf16[2048,32]{0,1:T(8,128)(2,1)S(1)} all-gather(bf16[256,32]{0,1:T(8,128)(2,1)S(1)} %multiply_convert_fusion), channel_id=1, replica_groups=mesh['owner'=4,'rows'=8] {'rows'}, dimensions={0}, use_global_device_ids=true | all-gather | bytes 147456 | tf_op jit(solution)/shard_map/all_gather | solution.py:30
  388.8 16.1 %all_gather.7 = bf16[2048,128]{0,1:T(8,128)(2,1)S(1)} all-gather(bf16[2048,32]{0,1:T(8,128)(2,1)S(1)} %all_gather.6), channel_id=1, replica_groups=mesh['owner'=4,'rows'=8] {'owner'}, dimensions={1}, use_global_device_ids=true | all-gather | bytes 655360 | tf_op jit(solution)/shard_map/all_gather | solution.py:31
  404.8 1.0 copy.28
  405.8 0.7 constant_dynamic-slice_fusion
  406.5 0.7 constant_dynamic-slice_fusion.1
  407.2 14.1 %copy.27 = bf16[32,8,256,96]{2,1,3,0:T(8,128)(2,1)} copy(bf16[32,8,256,96]{2,0,3,1:T(8,128)(2,1)} %bitcast.5) | data formatting | bytes 25165824 | tf_op jit(solution)/shard_map/all_to_all | solution.py:21
  421.2 19.5 %all_to_all.33 = bf16[32,2048,96]{1,2,0:T(8,128)(2,1)} reshape(bf16[32,8,256,96]{2,1,3,0:T(8,128)(2,1)} %copy.27) | data formatting | bytes 25165824 | tf_op jit(solution)/shard_map/all_to_all | solution.py:21
  440.7 14.1 %copy.23 = bf16[32,8,256,96]{2,1,3,0:T(8,128)(2,1)} copy(bf16[32,8,256,96]{2,0,3,1:T(8,128)(2,1)} %bitcast.2) | data formatting | bytes 25165824 | tf_op jit(solution)/shard_map/all_to_all | solution.py:20
  454.8 19.5 %all_to_all.29 = bf16[32,2048,96]{1,2,0:T(8,128)(2,1)} reshape(bf16[32,8,256,96]{2,1,3,0:T(8,128)(2,1)} %copy.23) | data formatting | bytes 25165824 | tf_op jit(solution)/shard_map/all_to_all | solution.py:20
  (8 shorter events, 0.0 us)
Async XLA Ops:
  7.2 74.2 %all-reduce.3.cloned.1.call-start = ((), (), s32[]{:S(2)}) async-start(), calls=%async_computation.2 | async-start | bytes 393216 | tf_op jit(solution)/shard_map/psum | solution.py:10
  96.5 144.4 %all-to-all-start.1 = ((bf16[32,256,768]{1,0,2:T(8,128)(2,1)}), bf16[32,256,768]{1,0,2:T(8,128)(2,1)}, u32[]{:S(2)}, u32[]{:S(2)}) async-start(bf16[32,256,768]{1,0,2:T(8,128)(2,1)} %divide_convert_fusion), calls=%async_computation.1 | async-start | bytes 25165824 | tf_op jit(solution)/shard_map/all_to_all | solution.py:21
  101.9 25.1 %copy-start = (f32[32,768]{1,0:T(8,128)S(1)}, f32[32,768]{1,0:T(8,128)}, u32[]{:S(2)}) copy-start(f32[32,768]{1,0:T(8,128)} %get-tuple-element.10) | copy-start | bytes 294916
  127.2 119.0 %copy-start.1 = (f32[256,32]{0,1:T(8,128)S(1)}, f32[256,32]{0,1:T(8,128)}, u32[]{:S(2)}) copy-start(f32[256,32]{0,1:T(8,128)} %param.6) | copy-start | bytes 98308
  127.3 119.0 %copy-start.2 = (f32[256]{0:T(256)S(1)}, f32[256]{0:T(256)}, u32[]{:S(2)}) copy-start(f32[256]{0:T(256)} %param.7) | copy-start | bytes 3076
  240.9 199.8 %all-to-all-start = ((bf16[32,256,768]{1,0,2:T(8,128)(2,1)}), bf16[32,256,768]{1,0,2:T(8,128)(2,1)}, u32[]{:S(2)}, u32[]{:S(2)}) async-start(bf16[32,256,768]{1,0,2:T(8,128)(2,1)} %divide_convert_fusion.1), calls=%async_computation | async-start | bytes 25165824 | tf_op jit(solution)/shard_map/all_to_all | solution.py:20
Sparse Core Ops, SparseCore 0:
  24.8 56.4 all-reduce.2
where the time goes:
time: 483 us; the launch traced here: 481 us
  blocking collectives  158 us (33%)
  waiting for transfers between devices  131 us (27%)
  local copies, waits for them, and re-layouts  120 us (25%)
  other arithmetic  46.6 us (10%)
  between operations  14.1 us (3%)
  starting transfers between devices  10.8 us (2%)
    all_gather x1, blocking collectives, on_device(): row_router = lax.all_gather(part_router, 'rows', axis=0, tiled=True)  142 us
    all_to_all x1, waiting for transfers between devices, on_device(): lax.all_to_all(narrow_up, 'rows', split_axis=2, concat_axis=1, tiled=True)  99.5 us
    unnamed x9, local copies, waits for them, and re-layouts  51.3 us
    all_to_all x2, local copies, waits for them, and re-layouts, on_device(): lax.all_to_all(narrow_gate, 'rows', split_axis=2, concat_axis=1, tiled=True)  33.6 us
    all_to_all x2, local copies, waits for them, and re-layouts, on_device(): lax.all_to_all(narrow_up, 'rows', split_axis=2, concat_axis=1, tiled=True)  33.6 us
    psum x1, waiting for transfers between devices, on_device(): lax.psum((jnp.sum(jnp.abs(w_gate), axis=1), jnp.sum(jnp.abs(w_up), axis=1...  31.5 us
    reduce_sum x1, other arithmetic, on_device(): jnp.sum(jnp.abs(w_up), axis=1)  17.4 us
    all_gather x1, blocking collectives, on_device(): serve_router = lax.all_gather(row_router, 'owner', axis=1, tiled=True)  16.1 us
  transfers between devices with their start and end apart: 3, of which 2 were waited for; matrix products, arithmetic and copies ran while one was open for 17% of the time, Pallas kernels for 0%

commit v1 on v0

--- a/solution.py
+++ b/solution.py
@@ -28,7 +28,7 @@
     )
     part_router = (router_weight * router_gain[:, None]).astype(jnp.bfloat16)
     row_router = lax.all_gather(part_router, "rows", axis=0, tiled=True)
-    serve_router = lax.all_gather(row_router, "owner", axis=1, tiled=True)
+    serve_router = jnp.concatenate(lax.all_gather(row_router, "owner"), axis=1)
     return (serve_gate, serve_up, scale_gate, scale_up, serve_router)
 
 

time: 483 us -> 484 us (level)
  no operation moved by 1% of the time
where the time goes in v1:
time: 484 us; the launch traced here: 482 us
  blocking collectives  158 us (33%)
  waiting for transfers between devices  131 us (27%)
  local copies, waits for them, and re-layouts  121 us (25%)
  other arithmetic  46.6 us (10%)
  between operations  14.1 us (3%)
  starting transfers between devices  10.8 us (2%)
    all_gather x1, blocking collectives, on_device(): row_router = lax.all_gather(part_router, 'rows', axis=0, tiled=True)  142 us
    all_to_all x1, waiting for transfers between devices, on_device(): lax.all_to_all(narrow_up, 'rows', split_axis=2, concat_axis=1, tiled=True)  99.5 us
    unnamed x9, local copies, waits for them, and re-layouts  51.3 us
    all_to_all x2, local copies, waits for them, and re-layouts, on_device(): lax.all_to_all(narrow_gate, 'rows', split_axis=2, concat_axis=1, tiled=True)  33.6 us
    all_to_all x2, local copies, waits for them, and re-layouts, on_device(): lax.all_to_all(narrow_up, 'rows', split_axis=2, concat_axis=1, tiled=True)  33.6 us
    psum x1, waiting for transfers between devices, on_device(): lax.psum((jnp.sum(jnp.abs(w_gate), axis=1), jnp.sum(jnp.abs(w_up), axis=1...  31.5 us
    reduce_sum x1, other arithmetic, on_device(): jnp.sum(jnp.abs(w_up), axis=1)  17.4 us
    all_gather x1, blocking collectives, on_device(): serve_router = jnp.concatenate(lax.all_gather(row_router, 'owner'), axis=1)  16.1 us
  transfers between devices with their start and end apart: 3, of which 2 were waited for; matrix products, arithmetic and copies ran while one was open for 17% of the time, Pallas kernels for 0%

profile of v1, /device:TPU:0, one launch (start us, length us, event | category | flops | bytes accessed | tf_op | source)
XLA Modules:
  0.0 481.8 jit_solution(18065938339496638089)
XLA Ops:
  7.2 0.0 all-reduce.3.cloned.1.call-start
  7.2 17.4 %abs_reduce_fusion = (f32[32,768]{1,0:T(8,128)}, f32[32,768]{1,0:T(8,128)}) fusion(f32[32,256,768]{2,1,0:T(8,128)} %param.5, f32[32,256,768]{2,1,0:T(8,128)} %param.4), kind=kLoop, calls=%fused_computation.1 | loop fusion | flops 25116672 | bytes 50528256 | tf_op jit(solution)/shard_map/reduce_sum | solution.py:11
  24.7 25.1 %copy.26 = f32[32,256,768]{1,0,2:T(8,128)} copy(f32[32,256,768]{2,1,0:T(8,128)} %param.5) | data formatting | bytes 50331648 | tf_op args[1]
  49.8 31.5 %all-reduce.3.cloned.1.call-done = (f32[32,768]{1,0:T(8,128)}, f32[32,768]{1,0:T(8,128)}) async-done(((f32[32,768]{1,0:T(8,128)}, f32[32,768]{1,0:T(8,128)}), (f32[32,768]{1,0:T(8,128)}, f32[32,768]{1,0:T(8,128)})) %all-reduce.3.cloned.1.call-update) | async-done | bytes 196624 | tf_op jit(solution)/shard_map/psum | solution.py:10
  81.3 0.9 broadcast_multiply_fusion
  82.2 0.2 copy.25
  82.4 14.1 %divide_convert_fusion = bf16[32,256,768]{1,0,2:T(8,128)(2,1)} fusion(f32[32,256,768]{1,0,2:T(8,128)} %copy.26, f32[32,768]{0,1:T(8,128)S(1)} %copy.25), kind=kLoop, calls=%fused_computation | loop fusion | flops 12582912 | bytes 37847040 | tf_op jit(solution)/shard_map/convert_element_type | solution.py:17
  96.5 5.4 %all-to-all-start.1 = ((bf16[32,256,768]{1,0,2:T(8,128)(2,1)}), bf16[32,256,768]{1,0,2:T(8,128)(2,1)}, u32[]{:S(2)}, u32[]{:S(2)}) async-start(bf16[32,256,768]{1,0,2:T(8,128)(2,1)} %divide_convert_fusion), calls=%async_computation.1 | async-start | bytes 25165824 | tf_op jit(solution)/shard_map/all_to_all | solution.py:21
  101.9 25.1 %copy.22 = f32[32,256,768]{1,0,2:T(8,128)} copy(f32[32,256,768]{2,1,0:T(8,128)} %param.4) | data formatting | bytes 50331648 | tf_op args[0]
  127.1 0.2 copy.21
  127.3 14.1 %divide_convert_fusion.1 = bf16[32,256,768]{1,0,2:T(8,128)(2,1)} fusion(f32[32,256,768]{1,0,2:T(8,128)} %copy.22, f32[32,768]{0,1:T(8,128)S(1)} %copy.21), kind=kLoop, calls=%fused_computation.2 | loop fusion | flops 12582912 | bytes 37847040 | tf_op jit(solution)/shard_map/convert_element_type | solution.py:16
  141.4 99.5 %all-to-all-done.1 = bf16[32,256,768]{1,0,2:T(8,128)(2,1)} async-done(((bf16[32,256,768]{1,0,2:T(8,128)(2,1)}), bf16[32,256,768]{1,0,2:T(8,128)(2,1)}, u32[]{:S(2)}, u32[]{:S(2)}) %all-to-all-start.1) | async-done | bytes 12582944 | tf_op jit(solution)/shard_map/all_to_all | solution.py:21
  240.9 5.4 %all-to-all-start = ((bf16[32,256,768]{1,0,2:T(8,128)(2,1)}), bf16[32,256,768]{1,0,2:T(8,128)(2,1)}, u32[]{:S(2)}, u32[]{:S(2)}) async-start(bf16[32,256,768]{1,0,2:T(8,128)(2,1)} %divide_convert_fusion.1), calls=%async_computation | async-start | bytes 25165824 | tf_op jit(solution)/shard_map/all_to_all | solution.py:20
  246.3 142.4 %all_gather.9 = bf16[2048,32]{0,1:T(8,128)(2,1)S(1)} all-gather(bf16[256,32]{0,1:T(8,128)(2,1)S(1)} %multiply_convert_fusion), channel_id=1, replica_groups=mesh['owner'=4,'rows'=8] {'rows'}, dimensions={0}, use_global_device_ids=true | all-gather | bytes 147456 | tf_op jit(solution)/shard_map/all_gather | solution.py:30
  388.8 16.1 %all-gather = bf16[8192,32]{0,1:T(8,128)(2,1)S(1)} all-gather(bf16[2048,32]{0,1:T(8,128)(2,1)S(1)} %all_gather.9), channel_id=2, replica_groups=mesh['owner'=4,'rows'=8] {'owner'}, dimensions={0}, use_global_device_ids=true | all-gather | bytes 655360 | tf_op jit(solution)/shard_map/all_gather | solution.py:31
  404.8 0.4 reshape.21
  405.2 0.3 copy.29
  405.5 1.0 copy.30
  406.5 0.7 constant_dynamic-slice_fusion
  407.2 0.7 constant_dynamic-slice_fusion.1
  407.8 14.1 %copy.28 = bf16[32,8,256,96]{2,1,3,0:T(8,128)(2,1)} copy(bf16[32,8,256,96]{2,0,3,1:T(8,128)(2,1)} %bitcast.5) | data formatting | bytes 25165824 | tf_op jit(solution)/shard_map/all_to_all | solution.py:21
  421.9 19.5 %all_to_all.33 = bf16[32,2048,96]{1,2,0:T(8,128)(2,1)} reshape(bf16[32,8,256,96]{2,1,3,0:T(8,128)(2,1)} %copy.28) | data formatting | bytes 25165824 | tf_op jit(solution)/shard_map/all_to_all | solution.py:21
  441.4 14.1 %copy.24 = bf16[32,8,256,96]{2,1,3,0:T(8,128)(2,1)} copy(bf16[32,8,256,96]{2,0,3,1:T(8,128)(2,1)} %bitcast.2) | data formatting | bytes 25165824 | tf_op jit(solution)/shard_map/all_to_all | solution.py:20
  455.5 19.5 %all_to_all.29 = bf16[32,2048,96]{1,2,0:T(8,128)(2,1)} reshape(bf16[32,8,256,96]{2,1,3,0:T(8,128)(2,1)} %copy.24) | data formatting | bytes 25165824 | tf_op jit(solution)/shard_map/all_to_all | solution.py:20
  (10 shorter events, 0.1 us)
Async XLA Ops:
  7.2 74.2 %all-reduce.3.cloned.1.call-start = ((), (), s32[]{:S(2)}) async-start(), calls=%async_computation.2 | async-start | bytes 393216 | tf_op jit(solution)/shard_map/psum | solution.py:10
  96.5 144.4 %all-to-all-start.1 = ((bf16[32,256,768]{1,0,2:T(8,128)(2,1)}), bf16[32,256,768]{1,0,2:T(8,128)(2,1)}, u32[]{:S(2)}, u32[]{:S(2)}) async-start(bf16[32,256,768]{1,0,2:T(8,128)(2,1)} %divide_convert_fusion), calls=%async_computation.1 | async-start | bytes 25165824 | tf_op jit(solution)/shard_map/all_to_all | solution.py:21
  101.9 25.1 %copy-start = (f32[32,768]{1,0:T(8,128)S(1)}, f32[32,768]{1,0:T(8,128)}, u32[]{:S(2)}) copy-start(f32[32,768]{1,0:T(8,128)} %get-tuple-element.20) | copy-start | bytes 294916
  127.2 119.0 %copy-start.1 = (f32[256,32]{0,1:T(8,128)S(1)}, f32[256,32]{0,1:T(8,128)}, u32[]{:S(2)}) copy-start(f32[256,32]{0,1:T(8,128)} %param.6) | copy-start | bytes 98308
  127.3 119.0 %copy-start.2 = (f32[256]{0:T(256)S(1)}, f32[256]{0:T(256)}, u32[]{:S(2)}) copy-start(f32[256]{0:T(256)} %param.7) | copy-start | bytes 3076
  240.9 200.5 %all-to-all-start = ((bf16[32,256,768]{1,0,2:T(8,128)(2,1)}), bf16[32,256,768]{1,0,2:T(8,128)(2,1)}, u32[]{:S(2)}, u32[]{:S(2)}) async-start(bf16[32,256,768]{1,0,2:T(8,128)(2,1)} %divide_convert_fusion.1), calls=%async_computation | async-start | bytes 25165824 | tf_op jit(solution)/shard_map/all_to_all | solution.py:20
Sparse Core Ops, SparseCore 0:
  24.8 56.4 all-reduce.2
